TPU v7x, 32 devices: a whole 2x2x4 slice. The times are simulated.
32 devices in a mesh: groups: 2 (over y), ctx: 4 (over z), role: 2 (over x), seq: 2 (over core).
Axes of the slice: x: 2, y: 2, z: 4, core: 2. Of those that a mesh axis runs over, the one named last changes fastest.
Arguments:
- queries: bfloat16 [32, 128, 576], P(('groups', 'role', 'seq'), 'ctx'), parts along dimension 0, may hold values from -24 to 24
- cache: bfloat16 [16, 4096, 576], P(('groups', 'role', 'seq'), 'ctx'), parts along dimension 0, may hold values from -4 to 4
- lengths: int32 [16], P(('groups', 'role', 'seq')), parts along dimension 0, may hold values from 4 to 4096, as said below
- positions: int32 [32], P(('groups', 'role', 'seq')), parts along dimension 0, may hold values from 0 to 4098, as said below
- value_up_weight: bfloat16 [128, 512, 128], P('ctx', ('role', 'seq')), may hold values from -0.25 to 0.25
- out_proj: bfloat16 [16384, 7168], P('ctx', ('role', 'seq')), may hold values from -0.046875 to 0.046875
- residual: bfloat16 [32, 7168], P('groups', ('role', 'seq')), parts along dimension 0, may hold values from -4 to 4
- norm_gain: float32 [7168], P(('role', 'seq')), may hold values from 0.5 to 1.5
- gate_weight: bfloat16 [7168, 9216], P(('role', 'seq'), 'ctx'), may hold values from -0.0625 to 0.0625
- up_weight: bfloat16 [7168, 9216], P(('role', 'seq'), 'ctx'), may hold values from -0.0625 to 0.0625
- down_weight: bfloat16 [9216, 7168], P('ctx', ('role', 'seq')), may hold values from -0.0625 to 0.0625
Outputs:
- layer_out: bfloat16 [32, 7168], P(('groups', 'ctx'), ('role', 'seq')), parts along dimension 0
There are 2 independent parts, one for each index of `groups`. A program takes and returns all parts, laid end to end along the dimension named above; an argument that names none is the same for every part. Nothing has to cross between parts.
Inputs may be any that keep to these rules, and one draw needn't show every extreme that they name: `lengths`: every sequence has at least 4 cached positions, and in every draw some sequence has all 4096. positions[r] lies between lengths[r // 2] - 4 and lengths[r // 2] + 2.
All inputs are finite; a program needn't handle non-finite values.
Results may differ from a plain program's by a relative error of at most 0.013.
Values may be sent and summed in bfloat16 or wider, within the bound.
A program may use at most 128 MiB of HBM per device.

v0:
```python
import jax
import jax.numpy as jnp
from jax import lax
from jax.sharding import PartitionSpec as P

D = 7168
HEADS = 128
LATENT = 512
ROPE = 64
VDIM = 128
MTP = 2
softmax_scale = 0.07216878364870323
epsilon = 1e-06


def settle_heads(pieces):
    maxima, totals, partial_value = pieces
    highest = jnp.max(maxima, axis=0)
    factor = jnp.exp(maxima - highest[None])
    denom = jnp.sum(factor * totals, axis=0)
    numer = jnp.sum(factor[..., None] * partial_value, axis=0)
    return (numer / denom[..., None]).astype(jnp.bfloat16)


def per_device(
    queries,
    cache,
    lengths,
    positions,
    value_up_weight,
    out_proj,
    residual,
    norm_gain,
    gate_weight,
    up_weight,
    down_weight,
):
    all_heads = lax.all_gather(queries, "ctx", axis=1, tiled=True)
    heads_here = queries.shape[1]
    width = LATENT + ROPE
    context_local = cache.shape[1]
    seq_here = cache.shape[0]
    offset = lax.axis_index("ctx") * context_local
    places = offset + jnp.arange(context_local, dtype=jnp.int32)
    maxima_list = []
    totals_list = []
    partial_list = []
    for number in range(seq_here):
        rows_pair = all_heads[MTP * number : MTP * (number + 1)].reshape(MTP * HEADS, width)
        keys_here = cache[number]
        limits = jnp.repeat(positions[MTP * number : MTP * (number + 1)], HEADS)
        length = lengths[number]

        def compute_block(rows_pair=rows_pair, keys_here=keys_here, limits=limits, length=length):
            scores = (
                jnp.dot(rows_pair, keys_here.T, preferred_element_type=jnp.float32) * softmax_scale
            )
            live = (places[None, :] < length) & (places[None, :] <= limits[:, None])
            block_max = jnp.max(jnp.where(live, scores, jnp.float32(-1e30)), axis=-1)
            probs = jnp.exp(
                jnp.where(live, scores - block_max[:, None], jnp.float32(-1e30))
            ).astype(jnp.bfloat16)
            block_weight_sum = jnp.sum(probs.astype(jnp.float32), axis=-1)
            block_out = jnp.dot(probs, keys_here[:, :LATENT], preferred_element_type=jnp.float32)
            return (block_max, block_weight_sum, block_out)

        block_max, block_weight_sum, block_out = compute_block()
        maxima_list.append(block_max.reshape(MTP, HEADS))
        totals_list.append(block_weight_sum.reshape(MTP, HEADS))
        partial_list.append(block_out.reshape(MTP, HEADS, LATENT))
    maxima = jnp.concatenate(maxima_list, axis=0)
    totals = jnp.concatenate(totals_list, axis=0)
    partial_value = jnp.concatenate(partial_list, axis=0)
    attended_values = settle_heads(
        (
            lax.all_to_all(maxima[None], "ctx", split_axis=2, concat_axis=0, tiled=True),
            lax.all_to_all(totals[None], "ctx", split_axis=2, concat_axis=0, tiled=True),
            lax.all_to_all(partial_value[None], "ctx", split_axis=2, concat_axis=0, tiled=True),
        )
    )
    mixed = jnp.einsum(
        "nut,utc->nuc",
        attended_values,
        lax.all_gather(value_up_weight, ("role", "seq"), axis=1, tiled=True),
        preferred_element_type=jnp.float32,
    )
    value_vectors = mixed.astype(jnp.bfloat16).reshape(attended_values.shape[0], heads_here * VDIM)
    per_head_terms = jnp.dot(
        lax.all_gather(value_vectors, ("role", "seq"), axis=0, tiled=True),
        out_proj,
        preferred_element_type=jnp.float32,
    )
    attn_out = lax.psum(per_head_terms, "ctx")
    resid = residual.astype(jnp.float32) + attn_out
    sumsq = lax.psum(jnp.sum(resid * resid, axis=1), ("role", "seq"))
    normed = (resid * lax.rsqrt(sumsq / D + epsilon)[:, None] * norm_gain[None, :]).astype(
        jnp.bfloat16
    )
    gate_term = jnp.dot(normed, gate_weight, preferred_element_type=jnp.float32)
    up_term = jnp.dot(normed, up_weight, preferred_element_type=jnp.float32)
    gate, up = lax.psum((gate_term, up_term), ("role", "seq"))
    hidden = (jax.nn.silu(gate) * up).astype(jnp.bfloat16)
    rows_here = resid.shape[0] // lax.axis_size("ctx")
    ffn_rows = lax.psum_scatter(
        jnp.dot(hidden, down_weight, preferred_element_type=jnp.float32),
        "ctx",
        scatter_dimension=0,
        tiled=True,
    )
    base_rows = lax.dynamic_slice_in_dim(resid, lax.axis_index("ctx") * rows_here, rows_here, 0)
    return (base_rows + ffn_rows).astype(jnp.bfloat16)


def solution(mesh):
    placed = (
        P(("groups", "role", "seq"), "ctx", None),
        P(("groups", "role", "seq"), "ctx", None),
        P(("groups", "role", "seq")),
        P(("groups", "role", "seq")),
        P("ctx", ("role", "seq"), None),
        P("ctx", ("role", "seq")),
        P("groups", ("role", "seq")),
        P(("role", "seq")),
        P(("role", "seq"), "ctx"),
        P(("role", "seq"), "ctx"),
        P("ctx", ("role", "seq")),
    )
    return jax.shard_map(
        per_device,
        mesh=mesh,
        in_specs=placed,
        out_specs=P(("groups", "ctx"), ("role", "seq")),
        check_vma=False,
    )
```

profile of v0, /device:TPU:0, one launch (start us, length us, event | category | flops | bytes accessed | tf_op | source)
XLA Modules:
  0.0 227.1 jit_solution(11326140525146923370)
XLA Ops:
  6.5 0.7 all-gather.3.cloned.1.call-update
  7.3 1.3 fusion.19
  8.6 1.3 fusion.12
  9.9 19.9 %all_gather.9 = bf16[4,128,576]{2,1,0:T(8,128)(2,1)S(1)} all-gather(bf16[4,32,576]{2,1,0:T(8,128)(2,1)} %param.11), channel_id=1, replica_groups=mesh['groups'=2,'ctx'=4,'role'=2,'seq'=2] {'ctx'}, dimensions={1}, use_global_device_ids=true | all-gather | bytes 737280 | tf_op jit(solution)/shard_map/all_gather | solution.py:38
  29.8 0.8 fusion.20
  30.7 1.8 convolution_multiply_fusion
  32.6 0.9 select_reduce_fusion.1
  33.5 0.9 convert_reduce_fusion.1
  34.4 0.1 copy.23
  34.5 0.6 broadcast.49
  35.1 0.8 reduce.1
  35.9 0.7 reshape.68
  36.6 3.8 %all-to-all-start.2 = ((f32[4,1,128]{2,1,0:T(1,128)}), f32[4,1,128]{2,1,0:T(1,128)S(1)}, u32[]{:S(2)}, u32[]{:S(2)}) async-start(f32[4,1,128]{2,1,0:T(1,128)} %reshape.68), calls=%async_computation.2 | async-start | bytes 4096 | tf_op jit(solution)/shard_map/all_to_all | solution.py:77
  40.4 0.2 slice_bitcast_fusion.1
  40.6 0.5 fusion.3
  41.1 0.5 fusion.1
  41.6 0.1 copy.18
  41.7 0.8 reduce.3
  42.5 0.7 reshape.66
  43.2 0.4 copy.20
  43.6 0.4 copy.21
  44.0 1.9 all-to-all-done.2
  45.9 3.2 %all-to-all-start = ((f32[4,1,128]{2,1,0:T(1,128)}), f32[4,1,128]{2,1,0:T(1,128)S(1)}, u32[]{:S(2)}, u32[]{:S(2)}) async-start(f32[4,1,128]{2,1,0:T(1,128)} %reshape.66), calls=%async_computation | async-start | bytes 4096 | tf_op jit(solution)/shard_map/all_to_all | solution.py:76
  49.1 1.4 maximum_bitcast_fusion
  50.6 4.1 %all-to-all-done = f32[4,1,128]{2,1,0:T(1,128)S(1)} async-done(((f32[4,1,128]{2,1,0:T(1,128)}), f32[4,1,128]{2,1,0:T(1,128)S(1)}, u32[]{:S(2)}, u32[]{:S(2)}) %all-to-all-start) | async-done | bytes 2080 | tf_op jit(solution)/shard_map/all_to_all | solution.py:76
  54.7 3.5 %all-to-all-start.1 = ((f32[1,4,128,512]{3,1,0,2:T(4,128)}), f32[1,4,128,512]{3,1,0,2:T(4,128)S(1)}, u32[]{:S(2)}, u32[]{:S(2)}) async-start(f32[1,4,128,512]{3,1,0,2:T(4,128)} %maximum_bitcast_fusion), calls=%async_computation.1 | async-start | bytes 2097152 | tf_op jit(solution)/shard_map/all_to_all | solution.py:78
  58.3 0.7 reduce.2
  58.9 0.1 reshape.69
  59.1 0.1 copy.24
  59.2 0.7 reduce.4
  59.8 0.1 reshape.67
  60.0 0.1 copy.19
  60.1 18.8 %all-to-all-done.1 = f32[1,4,128,512]{3,1,0,2:T(4,128)S(1)} async-done(((f32[1,4,128,512]{3,1,0,2:T(4,128)}), f32[1,4,128,512]{3,1,0,2:T(4,128)S(1)}, u32[]{:S(2)}, u32[]{:S(2)}) %all-to-all-start.1) | async-done | bytes 1048608 | tf_op jit(solution)/shard_map/all_to_all | solution.py:78
  78.9 0.3 fusion.5
  79.3 0.1 divide_convert_fusion
  79.4 2.8 %fusion = bf16[1,4,4096]{2,1,0:T(4,128)(2,1)S(1)} fusion(bf16[32,512,128]{2,1,0:T(8,128)(2,1)} %all-gather.3.cloned.1.call-done, bf16[4,32,512]{2,1,0:T(8,128)(2,1)S(1)} %divide_convert_fusion), kind=kOutput, calls=%fused_computation.5 | convolution fusion | flops 16793600 | bytes 4358144 | tf_op jit(solution)/shard_map/nut,utc->nuc/dot_general | solution.py:81
  82.2 5.4 %all-gather = bf16[4,4,4096]{2,1,0:T(4,128)(2,1)S(1)} all-gather(bf16[1,4,4096]{2,1,0:T(4,128)(2,1)S(1)} %fusion), channel_id=1, replica_groups=mesh['groups'=2,'ctx'=4,'role'=2,'seq'=2] {'role','seq'}, dimensions={0}, use_global_device_ids=true | all-gather | bytes 163840 | tf_op jit(solution)/shard_map/all_gather | solution.py:89
  87.7 7.8 %fusion.21 = f32[16,1792]{1,0:T(8,128)} fusion(bf16[16,4096]{1,0:T(8,128)(2,1)S(1)} %reshape.63, bf16[4096,1792]{1,0:T(8,128)(2,1)} %param.16), kind=kOutput, calls=%fused_computation.50 | convolution fusion | flops 234881024 | bytes 14925824 | tf_op jit(solution)/shard_map/dot_general | solution.py:88
  95.6 33.5 %all-reduce.6.cloned.1.call-done = f32[16,1792]{1,0:T(8,128)} async-done(((f32[16,1792]{1,0:T(8,128)}), f32[16,1792]{1,0:T(8,128)}) %all-reduce.6.cloned.1.call-update) | async-done | bytes 114704 | tf_op jit(solution)/shard_map/psum | solution.py:93
  129.1 1.0 multiply_reduce_fusion
  130.1 5.7 %psum.29 = f32[16]{0:T(128)S(1)} all-reduce(f32[16]{0:T(128)S(1)} %get-tuple-element.9), channel_id=1, replica_groups=mesh['groups'=2,'ctx'=4,'role'=2,'seq'=2] {'role','seq'}, use_global_device_ids=true, to_apply=%region_9.10 | all-reduce | flops 16 | bytes 128 | tf_op jit(solution)/shard_map/psum | solution.py:95
  135.8 5.2 %fusion.16 = f32[16,2304]{1,0:T(8,128)} fusion(bf16[1792,2304]{1,0:T(8,128)(2,1)} %param.19, f32[16,1792]{1,0:T(8,128)S(1)} %get-tuple-element.10, f32[1792]{0:T(1024)S(1)} %copy-done.1, f32[16]{0:T(128)S(1)} %add_rsqrt_fusion), kind=kOutput, calls=%fused_computation.46 | convolution fusion | flops 132206592 | bytes 8526912 | tf_op jit(solution)/shard_map/dot_general | solution.py:99
  141.1 5.3 %fusion.15 = f32[16,2304]{1,0:T(8,128)} fusion(bf16[1792,2304]{1,0:T(8,128)(2,1)} %param.20, f32[16,1792]{1,0:T(8,128)S(1)} %get-tuple-element.10, f32[1792]{0:T(1024)S(1)} %copy-done.1, f32[16]{0:T(128)S(1)} %add_rsqrt_fusion), kind=kOutput, calls=%fused_computation.45 | convolution fusion | flops 132206592 | bytes 8526912 | tf_op jit(solution)/shard_map/dot_general | solution.py:100
  146.4 32.9 %all-reduce.10.cloned.1.call-done = (f32[16,2304]{1,0:T(8,128)}, f32[16,2304]{1,0:T(8,128)}) async-done(((f32[16,2304]{1,0:T(8,128)}, f32[16,2304]{1,0:T(8,128)}), (f32[16,2304]{1,0:T(8,128)}, f32[16,2304]{1,0:T(8,128)})) %all-reduce.10.cloned.1.call-update) | async-done | bytes 294928 | tf_op jit(solution)/shard_map/psum | solution.py:101
  179.2 5.4 %fusion.7 = f32[16,1792]{1,0:T(8,128)} fusion(bf16[2304,1792]{1,0:T(8,128)(2,1)} %param.21, f32[16,2304]{1,0:T(8,128)} %get-tuple-element.7, f32[16,2304]{1,0:T(8,128)} %get-tuple-element.8), kind=kOutput, calls=%fused_computation.27 | convolution fusion | flops 132341760 | bytes 8667136 | tf_op jit(solution)/shard_map/dot_general | solution.py:105
  184.7 0.6 dynamic-slice
  185.9 33.3 %all-reduce.8.cloned.1.call-done = f32[16,1792]{1,0:T(8,128)} async-done(((f32[16,1792]{1,0:T(8,128)}), f32[16,1792]{1,0:T(8,128)}) %all-reduce.8.cloned.1.call-update) | async-done | bytes 114704
  219.2 1.4 fusion.9
  (25 shorter events, 0.5 us)
Async XLA Ops:
  6.5 26.1 %copy-start = (bf16[2,1024,576]{1,2,0:T(8,128)(2,1)S(1)}, bf16[2,1024,576]{1,2,0:T(8,128)(2,1)}, u32[]{:S(2)}) copy-start(bf16[2,1024,576]{1,2,0:T(8,128)(2,1)} %param.12) | copy-start | bytes 7077892
  6.5 72.8 %all-gather.3.cloned.1.call-start = ((), (), s32[]{:S(2)}) async-start(), calls=%async_computation.3 | async-start | bytes 5242880 | tf_op jit(solution)/shard_map/all_gather | solution.py:84
  36.6 9.3 %all-to-all-start.2 = ((f32[4,1,128]{2,1,0:T(1,128)}), f32[4,1,128]{2,1,0:T(1,128)S(1)}, u32[]{:S(2)}, u32[]{:S(2)}) async-start(f32[4,1,128]{2,1,0:T(1,128)} %reshape.68), calls=%async_computation.2 | async-start | bytes 4096 | tf_op jit(solution)/shard_map/all_to_all | solution.py:77
  45.9 8.8 %all-to-all-start = ((f32[4,1,128]{2,1,0:T(1,128)}), f32[4,1,128]{2,1,0:T(1,128)S(1)}, u32[]{:S(2)}, u32[]{:S(2)}) async-start(f32[4,1,128]{2,1,0:T(1,128)} %reshape.66), calls=%async_computation | async-start | bytes 4096 | tf_op jit(solution)/shard_map/all_to_all | solution.py:76
  54.7 24.2 %all-to-all-start.1 = ((f32[1,4,128,512]{3,1,0,2:T(4,128)}), f32[1,4,128,512]{3,1,0,2:T(4,128)S(1)}, u32[]{:S(2)}, u32[]{:S(2)}) async-start(f32[1,4,128,512]{3,1,0,2:T(4,128)} %maximum_bitcast_fusion), calls=%async_computation.1 | async-start | bytes 2097152 | tf_op jit(solution)/shard_map/all_to_all | solution.py:78
  58.2 70.9 %all-reduce.6.cloned.1.call-start = ((), (), s32[]{:S(2)}) async-start(), calls=%async_computation.4 | async-start | bytes 229376 | tf_op jit(solution)/shard_map/psum | solution.py:93
  87.7 41.4 %copy-start.2 = (bf16[16,1792]{1,0:T(8,128)(2,1)S(1)}, bf16[16,1792]{1,0:T(8,128)(2,1)}, u32[]{:S(2)}) copy-start(bf16[16,1792]{1,0:T(8,128)(2,1)} %param.17) | copy-start | bytes 172036
  87.7 48.1 %copy-start.1 = (f32[1792]{0:T(1024)S(1)}, f32[1792]{0:T(1024)}, u32[]{:S(2)}) copy-start(f32[1792]{0:T(1024)} %param.18) | copy-start | bytes 21508
  95.6 83.7 %all-reduce.10.cloned.1.call-start = ((), (), s32[]{:S(2)}) async-start(), calls=%async_computation.6 | async-start | bytes 589824 | tf_op jit(solution)/shard_map/psum | solution.py:101
  146.3 72.8 %all-reduce.8.cloned.1.call-start = ((), (), s32[]{:S(2)}) async-start(), calls=%async_computation.5 | async-start | bytes 229376
  179.2 5.4 %copy-start.3 = (u32[32]{0:T(128)S(1)}, u32[32]{0:T(128)}, u32[]{:S(2)}) copy-start(u32[32]{0:T(128)} %constant.35) | copy-start | bytes 388
Sparse Core Ops, SparseCore 0:
  8.9 37.1 all-gather.2
  95.7 33.3 all-reduce.5
  146.4 32.7 all-reduce.9
  184.8 34.3 all-reduce.7
where the time goes:
time: 228 us; the launch traced here: 227 us
  waiting for transfers between devices  125 us (55%)
  blocking collectives  31 us (14%)
  matrix products  30.3 us (13%)
  between operations  14 us (6%)
  starting transfers between devices  10.7 us (5%)
  other arithmetic  9.47 us (4%)
  local copies, waits for them, and re-layouts  6.56 us (3%)
    unnamed x5, waiting for transfers between devices  34 us
    psum x1, waiting for transfers between devices, per_device(): attn_out = lax.psum(per_head_terms, 'ctx')  33.5 us
    psum x1, waiting for transfers between devices, per_device(): gate, up = lax.psum((gate_term, up_term), ('role', 'seq'))  32.9 us
    all_gather x1, blocking collectives, per_device(): all_heads = lax.all_gather(queries, 'ctx', axis=1, tiled=True)  19.9 us
    all_to_all x1, waiting for transfers between devices, per_device(): lax.all_to_all(partial_value[None], 'ctx', split_axis=2, concat_axis=0, t...  18.8 us
    dot_general x1, matrix products, per_device(): jnp.dot(lax.all_gather(value_vectors, ('role', 'seq'), axis=0, tiled=True...  7.84 us
    psum x1, blocking collectives, per_device(): sumsq = lax.psum(jnp.sum(resid * resid, axis=1), ('role', 'seq'))  5.66 us
    all_gather x1, blocking collectives, per_device(): lax.all_gather(value_vectors, ('role', 'seq'), axis=0, tiled=True)  5.41 us
  transfers between devices with their start and end apart: 7, of which 6 were waited for; matrix products, arithmetic and copies ran while one was open for 8% of the time, Pallas kernels for 0%

commit v1 on v0

--- a/solution.py
+++ b/solution.py
@@ -90,7 +90,7 @@
         out_proj,
         preferred_element_type=jnp.float32,
     )
-    attn_out = lax.psum(per_head_terms, "ctx")
+    attn_out = jnp.sum(lax.all_gather(per_head_terms, "ctx"), axis=0)
     resid = residual.astype(jnp.float32) + attn_out
     sumsq = lax.psum(jnp.sum(resid * resid, axis=1), ("role", "seq"))
     normed = (resid * lax.rsqrt(sumsq / D + epsilon)[:, None] * norm_gain[None, :]).astype(

time: 228 us -> 207 us (0.908)
  waiting for transfers between devices: 125 us -> 90.3 us
  blocking collectives: 31 us -> 46.6 us
    psum x1 -> x0, waiting for transfers between devices: 33.5 us -> none  [per_device(): attn_out = lax.psum(per_head_terms, 'ctx')]
    all_gather x0 -> x1, blocking collectives: none -> 15.6 us  [per_device(): attn_out = jnp.sum(lax.all_gather(per_head_terms, 'ctx'), axis=0)]
    unnamed x5 -> x4, waiting for transfers between devices: 34 us -> 34 us
  transfers between devices with their start and end apart: 7 -> 6, of which waited for: 6 -> 5; matrix products, arithmetic and copies ran while one was open for 8% -> 8% of each run, Pallas kernels for 0% -> 0%
where the time goes in v1:
time: 207 us; the launch traced here: 206 us
  waiting for transfers between devices  90.3 us (44%)
  blocking collectives  46.6 us (23%)
  matrix products  29.6 us (14%)
  between operations  14 us (7%)
  starting transfers between devices  10.6 us (5%)
  other arithmetic  8.61 us (4%)
  local copies, waits for them, and re-layouts  6.56 us (3%)
    unnamed x4, waiting for transfers between devices  34 us
    psum x1, waiting for transfers between devices, per_device(): gate, up = lax.psum((gate_term, up_term), ('role', 'seq'))  31.5 us
    all_gather x1, blocking collectives, per_device(): all_heads = lax.all_gather(queries, 'ctx', axis=1, tiled=True)  19.9 us
    all_to_all x1, waiting for transfers between devices, per_device(): lax.all_to_all(partial_value[None], 'ctx', split_axis=2, concat_axis=0, t...  18.8 us
    all_gather x1, blocking collectives, per_device(): attn_out = jnp.sum(lax.all_gather(per_head_terms, 'ctx'), axis=0)  15.6 us
    dot_general x1, matrix products, per_device(): jnp.dot(lax.all_gather(value_vectors, ('role', 'seq'), axis=0, tiled=True...  7.19 us
    psum x1, blocking collectives, per_device(): sumsq = lax.psum(jnp.sum(resid * resid, axis=1), ('role', 'seq'))  5.66 us
    all_gather x1, blocking collectives, per_device(): lax.all_gather(value_vectors, ('role', 'seq'), axis=0, tiled=True)  5.41 us
  transfers between devices with their start and end apart: 6, of which 5 were waited for; matrix products, arithmetic and copies ran while one was open for 8% of the time, Pallas kernels for 0%

profile of v1, /device:TPU:0, one launch (start us, length us, event | category | flops | bytes accessed | tf_op | source)
XLA Modules:
  0.0 206.3 jit_solution(18373119654571800776)
XLA Ops:
  6.5 0.7 all-gather.4.cloned.1.call-update
  7.3 1.3 fusion.19
  8.6 1.3 fusion.12
  9.9 19.9 %all_gather.15 = bf16[4,128,576]{2,1,0:T(8,128)(2,1)S(1)} all-gather(bf16[4,32,576]{2,1,0:T(8,128)(2,1)} %param.11), channel_id=1, replica_groups=mesh['groups'=2,'ctx'=4,'role'=2,'seq'=2] {'ctx'}, dimensions={1}, use_global_device_ids=true | all-gather | bytes 737280 | tf_op jit(solution)/shard_map/all_gather | solution.py:38
  29.8 0.8 fusion.20
  30.7 1.8 convolution_multiply_fusion
  32.6 0.9 select_reduce_fusion.1
  33.5 0.9 convert_reduce_fusion.1
  34.4 0.1 copy.23
  34.5 0.6 broadcast.49
  35.1 0.8 reduce.1
  35.9 0.7 reshape.69
  36.6 3.8 %all-to-all-start.2 = ((f32[4,1,128]{2,1,0:T(1,128)}), f32[4,1,128]{2,1,0:T(1,128)S(1)}, u32[]{:S(2)}, u32[]{:S(2)}) async-start(f32[4,1,128]{2,1,0:T(1,128)} %reshape.69), calls=%async_computation.2 | async-start | bytes 4096 | tf_op jit(solution)/shard_map/all_to_all | solution.py:77
  40.4 0.2 slice_bitcast_fusion.1
  40.6 0.5 fusion.3
  41.1 0.5 fusion.1
  41.6 0.1 copy.18
  41.7 0.8 reduce.3
  42.5 0.7 reshape.67
  43.2 0.4 copy.20
  43.6 0.4 copy.21
  44.0 1.9 all-to-all-done.2
  45.9 3.2 %all-to-all-start = ((f32[4,1,128]{2,1,0:T(1,128)}), f32[4,1,128]{2,1,0:T(1,128)S(1)}, u32[]{:S(2)}, u32[]{:S(2)}) async-start(f32[4,1,128]{2,1,0:T(1,128)} %reshape.67), calls=%async_computation | async-start | bytes 4096 | tf_op jit(solution)/shard_map/all_to_all | solution.py:76
  49.1 1.4 maximum_bitcast_fusion
  50.6 4.1 %all-to-all-done = f32[4,1,128]{2,1,0:T(1,128)S(1)} async-done(((f32[4,1,128]{2,1,0:T(1,128)}), f32[4,1,128]{2,1,0:T(1,128)S(1)}, u32[]{:S(2)}, u32[]{:S(2)}) %all-to-all-start) | async-done | bytes 2080 | tf_op jit(solution)/shard_map/all_to_all | solution.py:76
  54.7 3.5 %all-to-all-start.1 = ((f32[1,4,128,512]{3,1,0,2:T(4,128)}), f32[1,4,128,512]{3,1,0,2:T(4,128)S(1)}, u32[]{:S(2)}, u32[]{:S(2)}) async-start(f32[1,4,128,512]{3,1,0,2:T(4,128)} %maximum_bitcast_fusion), calls=%async_computation.1 | async-start | bytes 2097152 | tf_op jit(solution)/shard_map/all_to_all | solution.py:78
  58.3 0.7 reduce.2
  58.9 0.1 reshape.70
  59.1 0.1 copy.24
  59.2 0.7 reduce.4
  59.8 0.1 reshape.68
  60.0 0.1 copy.19
  60.1 18.8 %all-to-all-done.1 = f32[1,4,128,512]{3,1,0,2:T(4,128)S(1)} async-done(((f32[1,4,128,512]{3,1,0,2:T(4,128)}), f32[1,4,128,512]{3,1,0,2:T(4,128)S(1)}, u32[]{:S(2)}, u32[]{:S(2)}) %all-to-all-start.1) | async-done | bytes 1048608 | tf_op jit(solution)/shard_map/all_to_all | solution.py:78
  78.9 0.3 fusion.5
  79.3 0.1 divide_convert_fusion
  79.4 2.8 %fusion = bf16[1,4,4096]{2,1,0:T(4,128)(2,1)S(1)} fusion(bf16[32,512,128]{2,1,0:T(8,128)(2,1)} %all-gather.4.cloned.1.call-done, bf16[4,32,512]{2,1,0:T(8,128)(2,1)S(1)} %divide_convert_fusion), kind=kOutput, calls=%fused_computation.5 | convolution fusion | flops 16793600 | bytes 4358144 | tf_op jit(solution)/shard_map/nut,utc->nuc/dot_general | solution.py:81
  82.2 5.4 %all-gather.1 = bf16[4,4,4096]{2,1,0:T(4,128)(2,1)S(1)} all-gather(bf16[1,4,4096]{2,1,0:T(4,128)(2,1)S(1)} %fusion), channel_id=1, replica_groups=mesh['groups'=2,'ctx'=4,'role'=2,'seq'=2] {'role','seq'}, dimensions={0}, use_global_device_ids=true | all-gather | bytes 163840 | tf_op jit(solution)/shard_map/all_gather | solution.py:89
  87.7 7.2 %fusion.21 = f32[16,1792]{1,0:T(8,128)S(1)} fusion(bf16[16,4096]{1,0:T(8,128)(2,1)S(1)} %reshape.64, bf16[4096,1792]{1,0:T(8,128)(2,1)} %param.16), kind=kOutput, calls=%fused_computation.50 | convolution fusion | flops 234881024 | bytes 14925824 | tf_op jit(solution)/shard_map/dot_general | solution.py:88
  94.9 15.6 %all-gather = f32[64,1792]{1,0:T(8,128)S(1)} all-gather(f32[16,1792]{1,0:T(8,128)S(1)} %fusion.21), channel_id=2, replica_groups=mesh['groups'=2,'ctx'=4,'role'=2,'seq'=2] {'ctx'}, dimensions={0}, use_global_device_ids=true | all-gather | bytes 573440 | tf_op jit(solution)/shard_map/all_gather | solution.py:93
  110.6 0.1 multiply_reduce_fusion
  110.7 5.7 %psum.21 = f32[16]{0:T(128)S(1)} all-reduce(f32[16]{0:T(128)S(1)} %get-tuple-element.9), channel_id=1, replica_groups=mesh['groups'=2,'ctx'=4,'role'=2,'seq'=2] {'role','seq'}, use_global_device_ids=true, to_apply=%region_9.10 | all-reduce | flops 16 | bytes 128 | tf_op jit(solution)/shard_map/psum | solution.py:95
  116.4 5.2 %fusion.16 = f32[16,2304]{1,0:T(8,128)} fusion(bf16[1792,2304]{1,0:T(8,128)(2,1)} %param.19, f32[16,1792]{1,0:T(8,128)S(1)} %get-tuple-element.10, f32[1792]{0:T(1024)S(1)} %copy-done.1, f32[16]{0:T(128)S(1)} %add_rsqrt_fusion), kind=kOutput, calls=%fused_computation.46 | convolution fusion | flops 132206592 | bytes 8526912 | tf_op jit(solution)/shard_map/dot_general | solution.py:99
  121.6 5.3 %fusion.15 = f32[16,2304]{1,0:T(8,128)} fusion(bf16[1792,2304]{1,0:T(8,128)(2,1)} %param.20, f32[16,1792]{1,0:T(8,128)S(1)} %get-tuple-element.10, f32[1792]{0:T(1024)S(1)} %copy-done.1, f32[16]{0:T(128)S(1)} %add_rsqrt_fusion), kind=kOutput, calls=%fused_computation.45 | convolution fusion | flops 132206592 | bytes 8526912 | tf_op jit(solution)/shard_map/dot_general | solution.py:100
  127.0 31.5 %all-reduce.7.cloned.1.call-done = (f32[16,2304]{1,0:T(8,128)}, f32[16,2304]{1,0:T(8,128)}) async-done(((f32[16,2304]{1,0:T(8,128)}, f32[16,2304]{1,0:T(8,128)}), (f32[16,2304]{1,0:T(8,128)}, f32[16,2304]{1,0:T(8,128)})) %all-reduce.7.cloned.1.call-update) | async-done | bytes 294928 | tf_op jit(solution)/shard_map/psum | solution.py:101
  158.5 5.4 %fusion.7 = f32[16,1792]{1,0:T(8,128)} fusion(bf16[2304,1792]{1,0:T(8,128)(2,1)} %param.21, f32[16,2304]{1,0:T(8,128)} %get-tuple-element.7, f32[16,2304]{1,0:T(8,128)} %get-tuple-element.8), kind=kOutput, calls=%fused_computation.27 | convolution fusion | flops 132341760 | bytes 8667136 | tf_op jit(solution)/shard_map/dot_general | solution.py:105
  163.9 0.6 dynamic-slice
  165.1 33.2 %all-reduce.5.cloned.1.call-done = f32[16,1792]{1,0:T(8,128)} async-done(((f32[16,1792]{1,0:T(8,128)}), f32[16,1792]{1,0:T(8,128)}) %all-reduce.5.cloned.1.call-update) | async-done | bytes 114704
  198.3 1.4 fusion.9
  (24 shorter events, 0.4 us)
Async XLA Ops:
  6.5 26.1 %copy-start = (bf16[2,1024,576]{1,2,0:T(8,128)(2,1)S(1)}, bf16[2,1024,576]{1,2,0:T(8,128)(2,1)}, u32[]{:S(2)}) copy-start(bf16[2,1024,576]{1,2,0:T(8,128)(2,1)} %param.12) | copy-start | bytes 7077892
  6.5 72.8 %all-gather.4.cloned.1.call-start = ((), (), s32[]{:S(2)}) async-start(), calls=%async_computation.3 | async-start | bytes 5242880 | tf_op jit(solution)/shard_map/all_gather | solution.py:84
  36.6 9.3 %all-to-all-start.2 = ((f32[4,1,128]{2,1,0:T(1,128)}), f32[4,1,128]{2,1,0:T(1,128)S(1)}, u32[]{:S(2)}, u32[]{:S(2)}) async-start(f32[4,1,128]{2,1,0:T(1,128)} %reshape.69), calls=%async_computation.2 | async-start | bytes 4096 | tf_op jit(solution)/shard_map/all_to_all | solution.py:77
  45.9 8.8 %all-to-all-start = ((f32[4,1,128]{2,1,0:T(1,128)}), f32[4,1,128]{2,1,0:T(1,128)S(1)}, u32[]{:S(2)}, u32[]{:S(2)}) async-start(f32[4,1,128]{2,1,0:T(1,128)} %reshape.67), calls=%async_computation | async-start | bytes 4096 | tf_op jit(solution)/shard_map/all_to_all | solution.py:76
  54.7 24.2 %all-to-all-start.1 = ((f32[1,4,128,512]{3,1,0,2:T(4,128)}), f32[1,4,128,512]{3,1,0,2:T(4,128)S(1)}, u32[]{:S(2)}, u32[]{:S(2)}) async-start(f32[1,4,128,512]{3,1,0,2:T(4,128)} %maximum_bitcast_fusion), calls=%async_computation.1 | async-start | bytes 2097152 | tf_op jit(solution)/shard_map/all_to_all | solution.py:78
  58.2 100.2 %all-reduce.7.cloned.1.call-start = ((), (), s32[]{:S(2)}) async-start(), calls=%async_computation.5 | async-start | bytes 589824 | tf_op jit(solution)/shard_map/psum | solution.py:101
  87.7 22.9 %copy-start.2 = (bf16[16,1792]{1,0:T(8,128)(2,1)S(1)}, bf16[16,1792]{1,0:T(8,128)(2,1)}, u32[]{:S(2)}) copy-start(bf16[16,1792]{1,0:T(8,128)(2,1)} %param.17) | copy-start | bytes 172036
  87.7 28.7 %copy-start.1 = (f32[1792]{0:T(1024)S(1)}, f32[1792]{0:T(1024)}, u32[]{:S(2)}) copy-start(f32[1792]{0:T(1024)} %param.18) | copy-start | bytes 21508
  126.9 71.4 %all-reduce.5.cloned.1.call-start = ((), (), s32[]{:S(2)}) async-start(), calls=%async_computation.4 | async-start | bytes 229376
  158.5 5.4 %copy-start.3 = (u32[32]{0:T(128)S(1)}, u32[32]{0:T(128)}, u32[]{:S(2)}) copy-start(u32[32]{0:T(128)} %constant.35) | copy-start | bytes 388
Sparse Core Ops, SparseCore 0:
  8.9 37.1 all-gather.3
  127.0 31.3 all-reduce.6
  164.0 34.3 all-reduce.4
